TPU v7x, 8 devices: a whole 2x2x1 slice. The times are simulated.
8 devices in a mesh: fsdp: 8 (over z, y, x, core).
Axes of the slice: x: 2, y: 2, z: 1, core: 2. Of those that a mesh axis runs over, the one named last changes fastest.
Arguments:
- resid_in: bfloat16 [16, 730, 1280], P('fsdp')
- grad_out: bfloat16 [16, 730, 1280], P('fsdp')
- ln1_gain: float32 [1280], P('fsdp')
- ln1_bias: float32 [1280], P('fsdp')
- qkv_weight: float32 [1280, 3840], P('fsdp')
- qkv_bias: float32 [3840], P('fsdp')
- out_weight: float32 [1280, 1280], P('fsdp')
- out_bias: float32 [1280], P('fsdp')
- ln2_gain: float32 [1280], P('fsdp')
- ln2_bias: float32 [1280], P('fsdp')
- fc_weight: float32 [1280, 5120], P('fsdp')
- fc_bias: float32 [5120], P('fsdp')
- proj_weight: float32 [5120, 1280], P('fsdp')
- proj_bias: float32 [1280], P('fsdp')
Outputs:
- output 1: bfloat16 [16, 730, 1280], P('fsdp')
- output 2: bfloat16 [16, 730, 1280], P('fsdp')
- output 3: float32 [1280], P('fsdp')
- output 4: float32 [1280], P('fsdp')
- output 5: float32 [1280, 3840], P('fsdp')
- output 6: float32 [3840], P('fsdp')
- output 7: float32 [1280, 1280], P('fsdp')
- output 8: float32 [1280], P('fsdp')
- output 9: float32 [1280], P('fsdp')
- output 10: float32 [1280], P('fsdp')
- output 11: float32 [1280, 5120], P('fsdp')
- output 12: float32 [5120], P('fsdp')
- output 13: float32 [5120, 1280], P('fsdp')
- output 14: float32 [1280], P('fsdp')
All inputs are finite; a program needn't handle non-finite values.
Results may differ from a plain program's by a relative error of at most 0.02.
Values are sent between devices in bfloat16 or wider.
A program may use at most 1 GiB of HBM per device.

v0:
```python
import math
import jax
import jax.numpy as jnp
from jax import lax
from jax.sharding import PartitionSpec as P

HEADS = 16
LN_EPS = 1e-5


def layer_norm_fwd(values, gain, bias):
    mean_val = jnp.mean(values, axis=-1, keepdims=True)
    centered = values - mean_val
    inv_std = lax.rsqrt(jnp.mean(centered * centered, axis=-1, keepdims=True) + LN_EPS)
    x_hat = centered * inv_std
    return x_hat * gain + bias, x_hat, inv_std


def layer_norm_bwd(grad_norm, x_hat, inv_std, gain):
    grad_hat = grad_norm * gain
    grad_vals = inv_std * (grad_hat - jnp.mean(grad_hat, axis=-1, keepdims=True)
                           - x_hat * jnp.mean(grad_hat * x_hat, axis=-1, keepdims=True))
    return grad_vals, jnp.sum(grad_norm * x_hat, axis=(0, 1)), jnp.sum(grad_norm, axis=(0, 1))


def forward_local(full, tokens):
    (ln1_gain, ln1_bias, qkv_weight, qkv_bias, out_weight, out_bias,
     ln2_gain, ln2_bias, fc_weight, fc_bias, proj_weight, proj_bias) = full
    images, seq_len, width = tokens.shape
    head_dim = width // HEADS
    resid = tokens.astype(jnp.float32)
    normed, hat_one, inv_one = layer_norm_fwd(resid, ln1_gain, ln1_bias)
    normed_one = normed.astype(jnp.bfloat16)
    qkv_vals = (jnp.einsum("bsw,wk->bsk", normed_one, qkv_weight, preferred_element_type=jnp.float32) + qkv_bias).astype(jnp.bfloat16)
    qkv_vals = qkv_vals.reshape(images, seq_len, 3, HEADS, head_dim)
    query_heads = qkv_vals[:, :, 0]
    key_heads = qkv_vals[:, :, 1]
    value_heads = qkv_vals[:, :, 2]
    scores = jnp.einsum("bqhd,bkhd->bhqk", query_heads, key_heads, preferred_element_type=jnp.float32) * (head_dim ** -0.5)
    attn_probs = jax.nn.softmax(scores, axis=-1)
    probs_low = attn_probs.astype(jnp.bfloat16)
    mixed = jnp.einsum("bhqk,bkhd->bqhd", probs_low, value_heads, preferred_element_type=jnp.float32).astype(jnp.bfloat16).reshape(images, seq_len, width)
    middle = (resid + jnp.einsum("bsw,wv->bsv", mixed, out_weight, preferred_element_type=jnp.float32) + out_bias).astype(jnp.bfloat16)
    middle_wide = middle.astype(jnp.float32)
    normed, hat_two, inv_two = layer_norm_fwd(middle_wide, ln2_gain, ln2_bias)
    normed_two = normed.astype(jnp.bfloat16)
    pre_act = jnp.einsum("bsw,wf->bsf", normed_two, fc_weight, preferred_element_type=jnp.float32) + fc_bias
    hidden = jax.nn.gelu(pre_act, approximate=False).astype(jnp.bfloat16)
    resid_out = (middle_wide + jnp.einsum("bsf,fw->bsw", hidden, proj_weight, preferred_element_type=jnp.float32) + proj_bias).astype(jnp.bfloat16)
    saved = (hat_one, inv_one, normed_one, query_heads, key_heads, value_heads, attn_probs, probs_low,
             mixed, hat_two, inv_two, normed_two, pre_act, hidden)
    return resid_out, saved


def backward_local(weights, saved, grad_out):
    (ln1_gain, qkv_weight, out_weight, ln2_gain, fc_weight, proj_weight) = weights
    (hat_one, inv_one, normed_one, query_heads, key_heads, value_heads, attn_probs, probs_low,
     mixed, hat_two, inv_two, normed_two, pre_act, hidden) = saved
    images, seq_len, width = grad_out.shape
    head_dim = width // HEADS
    grad_wide = grad_out.astype(jnp.float32)
    d_proj_weight = jnp.einsum("bsf,bsw->fw", hidden, grad_out, preferred_element_type=jnp.float32)
    d_proj_bias = jnp.sum(grad_wide, axis=(0, 1))
    grad_hidden = jnp.einsum("bsw,fw->bsf", grad_out, proj_weight, preferred_element_type=jnp.float32)
    gauss_cdf = 0.5 * (1.0 + lax.erf(pre_act * (0.5 ** 0.5)))
    gauss_pdf = jnp.exp(-0.5 * pre_act * pre_act) * ((2.0 * math.pi) ** -0.5)
    grad_pre = grad_hidden * (gauss_cdf + pre_act * gauss_pdf)
    grad_pre_low = grad_pre.astype(jnp.bfloat16)
    d_fc_weight = jnp.einsum("bsw,bsf->wf", normed_two, grad_pre_low, preferred_element_type=jnp.float32)
    d_fc_bias = jnp.sum(grad_pre, axis=(0, 1))
    grad_norm = jnp.einsum("bsf,wf->bsw", grad_pre_low, fc_weight, preferred_element_type=jnp.float32)
    grad_ln, d_ln2_gain, d_ln2_bias = layer_norm_bwd(grad_norm, hat_two, inv_two, ln2_gain)
    grad_middle = grad_wide + grad_ln
    grad_middle_low = grad_middle.astype(jnp.bfloat16)
    d_out_weight = jnp.einsum("bsw,bsv->wv", mixed, grad_middle_low, preferred_element_type=jnp.float32)
    d_out_bias = jnp.sum(grad_middle, axis=(0, 1))
    grad_mixed = jnp.einsum("bsv,wv->bsw", grad_middle_low, out_weight, preferred_element_type=jnp.float32)
    grad_mixed = grad_mixed.astype(jnp.bfloat16).reshape(images, seq_len, HEADS, head_dim)
    grad_probs = jnp.einsum("bqhd,bkhd->bhqk", grad_mixed, value_heads, preferred_element_type=jnp.float32)
    grad_value = jnp.einsum("bhqk,bqhd->bkhd", probs_low, grad_mixed, preferred_element_type=jnp.float32)
    grad_scores = attn_probs * (grad_probs - jnp.sum(grad_probs * attn_probs, axis=-1, keepdims=True)) * (head_dim ** -0.5)
    grad_scores = grad_scores.astype(jnp.bfloat16)
    grad_query = jnp.einsum("bhqk,bkhd->bqhd", grad_scores, key_heads, preferred_element_type=jnp.float32)
    grad_key = jnp.einsum("bhqk,bqhd->bkhd", grad_scores, query_heads, preferred_element_type=jnp.float32)
    grad_qkv = jnp.stack([grad_query, grad_key, grad_value], axis=2).reshape(images, seq_len, 3 * width)
    grad_qkv_low = grad_qkv.astype(jnp.bfloat16)
    d_qkv_weight = jnp.einsum("bsw,bsk->wk", normed_one, grad_qkv_low, preferred_element_type=jnp.float32)
    d_qkv_bias = jnp.sum(grad_qkv, axis=(0, 1))
    grad_norm = jnp.einsum("bsk,wk->bsw", grad_qkv_low, qkv_weight, preferred_element_type=jnp.float32)
    grad_ln, d_ln1_gain, d_ln1_bias = layer_norm_bwd(grad_norm, hat_one, inv_one, ln1_gain)
    grad_in = (grad_middle + grad_ln).astype(jnp.bfloat16)
    return grad_in, (d_ln1_gain, d_ln1_bias, d_qkv_weight, d_qkv_bias, d_out_weight, d_out_bias,
                     d_ln2_gain, d_ln2_bias, d_fc_weight, d_fc_bias, d_proj_weight, d_proj_bias)


def solution(mesh):
    specs = (P("fsdp"),) * 14

    def gather_bf16(shards):
        return tuple(lax.all_gather(shard.astype(jnp.bfloat16), "fsdp", axis=0, tiled=True) for shard in shards)

    def device_step(resid_in, grad_out, *shards):
        full = gather_bf16(shards)
        resid_out, saved = forward_local(full, resid_in)
        needed, resid_out = lax.optimization_barrier(
            ((shards[0], shards[2], shards[4], shards[6], shards[8], shards[10]), resid_out))
        weights = gather_bf16(needed)
        grad_in, grads = backward_local(weights, saved, grad_out)
        grad_shards = tuple(lax.psum_scatter(grad, "fsdp", scatter_dimension=0, tiled=True) for grad in grads)
        return (resid_out, grad_in) + grad_shards

    return jax.shard_map(device_step, mesh=mesh, in_specs=specs, out_specs=specs, check_vma=False)
```

profile of v0, /device:TPU:0, one launch (start us, length us, event | category | flops | bytes accessed | tf_op | source)
XLA Modules:
  0.0 1349.8 jit_solution(15256269222029268208)
XLA Ops:
  24.7 26.2 %all-reduce.19 = (bf16[3840]{0:T(1024)(128)(2,1)S(1)}, bf16[1280]{0:T(1024)(128)(2,1)S(1)}, bf16[1280]{0:T(1024)(128)(2,1)S(1)}, bf16[1280]{0:T(1024)(128)(2,1)S...) all-reduce(bf16[3840]{0:T(1024)(128)(2,1)S(1)} %dynamic-update-slic, ...), channel_id=1, replica_groups=mesh['fsdp'=8] {'fsdp'}, use_global_device_ids=true, to_apply=%add.2 | all-reduce | flops 11520 | bytes 46080
  69.5 22.2 %add_convert_fusion = bf16[2,730,3840]{2,1,0:T(8,128)(2,1)} fusion(f32[3840]{0:T(1024)S(1)} %convert_element_type.149, bf16[1280,3840]{1,0:T(8,128)(2,1)} %all-gather.10.cloned.1.call-done, f32[1280]{0:T(1024)S(1)} %convert_element_type.145, f32[1280]{0:T(1024)S(1)} %convert_element_type.143, f32[2,730]{1,0:T(2,128)S(1)} %add_rsqrt_fusion.1, ...), kind=kOutput, calls=%fused_computation.41 | convolution fusion | flops 14374809600 | bytes 24818080 | tf_op jit(solution)/shard_map/bsw,wk->bsk/dot_general | solution.py:34
  91.7 16.0 %copy.66 = bf16[2,730,3840]{1,2,0:T(8,128)(2,1)} copy(bf16[2,730,3840]{2,1,0:T(8,128)(2,1)} %add_convert_fusion) | data formatting | bytes 22425600 | tf_op jit(solution)/shard_map/convert_element_type | solution.py:34
  107.6 31.9 %fusion.120 = (f32[2,16,730]{2,1,0:T(8,128)S(1)}, f32[2,16,730,730]{2,3,1,0:T(8,128)}) fusion(bf16[2,730,3,16,80]{1,4,3,2,0:T(8,128)(2,1)} %bitcast.119), kind=kOutput, calls=%fused_computation.142 | convolution fusion | flops 2779606784 | bytes 76168960 | tf_op jit(solution)/shard_map/sub | solution.py:40
  139.5 26.9 %fusion.101 = bf16[2,16,80,730]{3,2,1,0:T(8,128)(2,1)} fusion(bf16[2,730,3,16,80]{1,4,3,2,0:T(8,128)(2,1)} %bitcast.120, f32[2,16,730,730]{2,3,1,0:T(8,128)} %get-tuple-element.101, f32[2,16,730]{2,1,0:T(8,128)S(1)} %get-tuple-element.100), kind=kOutput, calls=%fused_computation.121 | convolution fusion | flops 2764422400 | bytes 80114944 | tf_op jit(solution)/shard_map/bhqk,bkhd->bqhd/dot_general | solution.py:42
  179.5 40.4 %fusion.83 = (u8[730,5120]{1,0:T(8,128)(4,1)}, u8[730,5120]{1,0:T(8,128)(4,1)}, f32[2,730,5120]{2,1,0:T(8,128)}) fusion(f32[5120]{0:T(1024)S(1)} %bitcast.128, bf16[1280,5120]{1,0:T(8,128)(2,1)} %all-gather.14.cloned.1.call-done, bf16[2,730,1280]{2,1,0:T(8,128)(2,1)} %copy-done, f32[1280]{0:T(1024)S(1)} %copy-done.16, f32[1280]{0:T(1024)S(1)} %copy-done.18, ...), kind=kOutput, calls=%fused_computation.106 | convolution fusion | flops 19244902400 | bytes 54263200 | tf_op jit(solution)/shard_map/bsw,wf->bsf/dot_general | solution.py:47
  219.9 73.2 %fusion.11 = bf16[2,730,5120]{2,1,0:T(8,128)(2,1)} fusion(f32[2,730,5120]{2,1,0:T(8,128)} %get-tuple-element.104, f32[5120]{0:T(1024)S(1)} %bitcast.129, u8[730,5120]{1,0:T(8,128)(4,1)} %get-tuple-element.71, u8[730,5120]{1,0:T(8,128)(4,1)} %get-tuple-element.70), kind=kLoop, calls=%fused_computation.14 | loop fusion | flops 530739200 | bytes 52346880 | tf_op jit(solution)/shard_map/convert_element_type | solution.py:48
  293.2 27.4 %fusion.79 = bf16[2,730,1280]{2,1,0:T(8,128)(2,1)} fusion(bf16[2,730,1280]{2,1,0:T(8,128)(2,1)} %copy-done, bf16[2,730,5120]{2,1,0:T(8,128)(2,1)} %fusion.11, bf16[5120,1280]{1,0:T(8,128)(2,1)} %all-gather.16.cloned.1.call-done, f32[1280]{0:T(1024)S(1)} %copy-done.24), kind=kOutput, calls=%fused_computation.102 | convolution fusion | flops 19143983104 | bytes 35537920 | tf_op jit(solution)/shard_map/bsf,fw->bsw/dot_general | solution.py:49
  327.9 23.0 %all-reduce.18 = (bf16[1280]{0:T(1024)(128)(2,1)S(1)}, bf16[1280]{0:T(1024)(128)(2,1)S(1)}) all-reduce(bf16[1280]{0:T(1024)(128)(2,1)S(1)} %dynamic-update-slice.7, bf16[1280]{0:T(1024)(128)(2,1)S(1)} %dynamic-update-slice.8), channel_id=1, replica_groups=mesh['fsdp'=8] {'fsdp'}, use_global_device_ids=true, to_apply=%add.7 | all-reduce | flops 2560 | bytes 10240
  354.4 37.4 %all-gather.18.cloned.1.call-done = bf16[5120,1280]{1,0:T(8,128)(2,1)} async-done(((bf16[640,1280]{1,0:T(8,128)(2,1)}), bf16[5120,1280]{1,0:T(8,128)(2,1)}) %all-gather.18.cloned.1.call-update) | async-done | bytes 13107216 | tf_op jit(solution)/shard_map/all_gather | solution.py:100
  391.9 38.3 %fusion.121 = (f32[5120]{0:T(1024)}, bf16[2,730,5120]{2,1,0:T(8,128)(2,1)}) fusion(f32[2,730,5120]{2,1,0:T(8,128)} %get-tuple-element.104, f32[5120]{0:T(1024)S(1)} %bitcast.130, bf16[2,730,1280]{2,0,1:T(2,128)(2,1)} %param.15, bf16[5120,1280]{1,0:T(8,128)(2,1)} %all-gather.18.cloned.1.call-done), kind=kOutput, calls=%fused_computation.143 | convolution fusion | flops 19226210304 | bytes 61736960 | tf_op jit(solution)/shard_map/bsw,fw->bsf/dot_general | solution.py:64
  430.2 32.4 %all-gather.20.cloned.1.call-done = bf16[1280,5120]{1,0:T(8,128)(2,1)} async-done(((bf16[160,5120]{1,0:T(8,128)(2,1)}), bf16[1280,5120]{1,0:T(8,128)(2,1)}) %all-gather.20.cloned.1.call-update) | async-done | bytes 13107216 | tf_op jit(solution)/shard_map/all_gather | solution.py:100
  462.7 31.6 %fusion.65 = (f32[1280]{0:T(1024)}, f32[2,730]{1,0:T(2,128)S(1)}, f32[2,730]{1,0:T(2,128)S(1)}, f32[1280]{0:T(1024)}, f32[2,730,1280]{2,1,0:T(8,128)S(1)}) fusion(bf16[2,730,1280]{2,1,0:T(8,128)(2,1)} %copy-done, f32[2,730]{1,0:T(2,128)S(1)} %add_rsqrt_fusion, f32[2,730]{1,0:T(2,128)S(1)} %broadcast_multiply_fusion.4, f32[1280]{0:T(1024)S(1)} %convert_element_type.177, ...), kind=kOutput, calls=%fused_computation.88 | convolution fusion | flops 19155189760 | bytes 39309120 | tf_op jit(solution)/shard_map/bsf,wf->bsw/dot_general | solution.py:71
  516.7 28.2 %fusion.88 = f32[2,16,730,730]{2,3,1,0:T(8,128)} fusion(bf16[2,730,16,80]{1,3,2,0:T(8,128)(2,1)} %bitcast.124, bf16[2,730,3,16,80]{1,4,3,2,0:T(8,128)(2,1)} %bitcast.121), kind=kOutput, calls=%fused_computation.114 | convolution fusion | flops 2728448000 | bytes 76075520 | tf_op jit(solution)/shard_map/bqhd,bkhd->bhqk/dot_general | solution.py:79
  544.8 91.0 %fusion.94 = f32[2,730,1,16,80]{1,4,3,0,2:T(8,128)} fusion(f32[2,16,730,730]{2,3,1,0:T(8,128)} %fusion.88, bf16[2,730,3,16,80]{1,4,3,2,0:T(8,128)(2,1)} %bitcast.122, f32[2,16,730,730]{2,3,1,0:T(8,128)} %get-tuple-element.101, f32[2,16,730]{2,1,0:T(8,128)S(1)} %copy-done.39), kind=kOutput, calls=%fused_computation.118 | convolution fusion | flops 2847841792 | bytes 301010944 | tf_op jit(solution)/shard_map/bhqk,bkhd->bqhd/dot_general | solution.py:83
  635.9 90.9 %fusion.97 = f32[2,730,1,16,80]{1,4,3,0,2:T(8,128)} fusion(f32[2,16,730,730]{2,3,1,0:T(8,128)} %fusion.88, bf16[2,730,3,16,80]{1,4,3,2,0:T(8,128)(2,1)} %bitcast.123, f32[2,16,730,730]{2,3,1,0:T(8,128)} %get-tuple-element.101, f32[2,16,730]{2,1,0:T(8,128)S(1)} %copy-done.39), kind=kOutput, calls=%fused_computation.119 | convolution fusion | flops 2847841792 | bytes 301010944 | tf_op jit(solution)/shard_map/bhqk,bqhd->bkhd/dot_general | solution.py:84
  726.7 29.2 %fusion.91 = f32[2,730,1,16,80]{1,4,3,0,2:T(8,128)} fusion(bf16[2,730,16,80]{1,3,2,0:T(8,128)(2,1)} %bitcast.125, f32[2,16,730,730]{2,3,1,0:T(8,128)} %get-tuple-element.101, f32[2,16,730]{2,1,0:T(8,128)S(1)} %copy-done.39), kind=kOutput, calls=%fused_computation.117 | convolution fusion | flops 2762553600 | bytes 79517440 | tf_op jit(solution)/shard_map/bhqk,bqhd->bkhd/dot_general | solution.py:80
  780.2 26.2 %fusion.74 = (f32[1280]{0:T(1024)}, f32[2,730]{1,0:T(2,128)}, f32[2,730]{1,0:T(2,128)}, f32[1280]{0:T(1024)}, f32[2,730,1280]{2,1,0:T(8,128)}) fusion(f32[2,730]{1,0:T(2,128)S(1)} %copy-done.15, f32[2,730]{1,0:T(2,128)S(1)} %copy-done.9, bf16[2,730,1280]{2,0,1:T(2,128)(2,1)} %param.14, f32[1280]{0:T(1024)S(1)} %copy-done.10, ...), kind=kOutput, calls=%fused_computation.97 | convolution fusion | flops 14371067904 | bytes 32294720 | tf_op jit(solution)/shard_map/bsk,wk->bsw/dot_general | solution.py:89
  817.6 27.6 %convolution_bitcast_fusion = f32[5120,1280]{1,0:T(8,128)} fusion(bf16[2,730,5120]{2,1,0:T(8,128)(2,1)} %fusion.11, bf16[2,730,1280]{2,0,1:T(2,128)(2,1)} %param.15), kind=kOutput, calls=%fused_computation.42 | convolution fusion | flops 19136512000 | bytes 44902400 | tf_op jit(solution)/shard_map/bsf,bsw->fw/dot_general | solution.py:62
  845.9 24.2 %convolution_bitcast_fusion.2 = f32[1280,3840]{1,0:T(8,128)} fusion(bf16[2,730,3840]{1,2,0:T(8,128)(2,1)} %bitcast.127, f32[1280]{0:T(1024)S(1)} %copy-done.21, f32[1280]{0:T(1024)S(1)} %copy-done.23, f32[2,730]{1,0:T(2,128)S(1)} %copy-done.15, f32[2,730]{1,0:T(2,128)S(1)} %copy-done.9, bf16[2,730,1280]{2,0,1:T(2,128)(2,1)} %param.14), kind=kOutput, calls=%fused_computation.48 | convolution fusion | flops 14363596800 | bytes 34633120 | tf_op jit(solution)/shard_map/bsw,bsk->wk/dot_general | solution.py:87
  870.9 28.9 %convolution_bitcast_fusion.1 = f32[1280,5120]{1,0:T(8,128)} fusion(bf16[2,730,5120]{2,1,0:T(8,128)(2,1)} %get-tuple-element.108, bf16[2,730,1280]{2,1,0:T(8,128)(2,1)} %copy-done, f32[1280]{0:T(1024)S(1)} %copy-done.17, f32[1280]{0:T(1024)S(1)} %copy-done.19, f32[2,730]{1,0:T(2,128)S(1)} %copy-done.13, f32[2,730]{1,0:T(2,128)S(1)} %copy-done.7), kind=kOutput, calls=%fused_computation.43 | convolution fusion | flops 19147724800 | bytes 44924320 | tf_op jit(solution)/shard_map/bsw,bsf->wf/dot_general | solution.py:69
  932.0 131.0 %reduce-scatter.11.cloned.1.call-done = f32[640,1280]{1,0:T(8,128)} async-done(((f32[5120,1280]{1,0:T(8,128)}), f32[640,1280]{1,0:T(8,128)}) %reduce-scatter.11.cloned.1.call-update) | async-done | bytes 3276816 | tf_op jit(solution)/shard_map/reduce_scatter | solution.py:109
  1063.0 124.6 %reduce-scatter.5.cloned.1.call-done = f32[160,3840]{1,0:T(8,128)} async-done(((f32[1280,3840]{1,0:T(8,128)}), f32[160,3840]{1,0:T(8,128)}) %reduce-scatter.5.cloned.1.call-update) | async-done | bytes 2457616 | tf_op jit(solution)/shard_map/reduce_scatter | solution.py:109
  1187.6 155.4 %reduce-scatter.9.cloned.1.call-done = f32[160,5120]{1,0:T(8,128)} async-done(((f32[1280,5120]{1,0:T(8,128)}), f32[160,5120]{1,0:T(8,128)}) %reduce-scatter.9.cloned.1.call-update) | async-done | bytes 3276816 | tf_op jit(solution)/shard_map/reduce_scatter | solution.py:109
  (192 shorter events, 150.8 us)
Async XLA Ops:
  7.3 62.2 %all-gather.10.cloned.1.call-start = ((), (), s32[]{:S(2)}) async-start(), calls=%async_computation.4 | async-start | bytes 11059200 | tf_op jit(solution)/shard_map/all_gather | solution.py:100
  10.3 156.1 %all-gather.12.cloned.1.call-start = ((), (), s32[]{:S(2)}) async-start(), calls=%async_computation.5 | async-start | bytes 3686400 | tf_op jit(solution)/shard_map/all_gather | solution.py:100
  12.4 167.1 %all-gather.14.cloned.1.call-start = ((), (), s32[]{:S(2)}) async-start(), calls=%async_computation.6 | async-start | bytes 14745600 | tf_op jit(solution)/shard_map/all_gather | solution.py:100
  15.7 277.4 %all-gather.16.cloned.1.call-start = ((), (), s32[]{:S(2)}) async-start(), calls=%async_computation.7 | async-start | bytes 14745600 | tf_op jit(solution)/shard_map/all_gather | solution.py:100
  17.1 374.7 %all-gather.18.cloned.1.call-start = ((), (), s32[]{:S(2)}) async-start(), calls=%async_computation.8 | async-start | bytes 14745600 | tf_op jit(solution)/shard_map/all_gather | solution.py:100
  19.9 71.8 %copy-start.8 = (f32[2,730]{1,0:T(2,128)}, f32[2,730]{1,0:T(2,128)S(1)}, u32[]{:S(2)}) copy-start(f32[2,730]{1,0:T(2,128)S(1)} %broadcast_multiply_fusion.5) | copy-start | bytes 17524
  23.1 68.6 %copy-start.14 = (f32[2,730]{1,0:T(2,128)}, f32[2,730]{1,0:T(2,128)S(1)}, u32[]{:S(2)}) copy-start(f32[2,730]{1,0:T(2,128)S(1)} %add_rsqrt_fusion.1) | copy-start | bytes 17524
  50.9 40.8 %copy-start.20 = (f32[1280]{0:T(1024)}, f32[1280]{0:T(1024)S(1)}, u32[]{:S(2)}) copy-start(f32[1280]{0:T(1024)S(1)} %convert_element_type.145) | copy-start | bytes 15364
  50.9 40.8 %copy-start.22 = (f32[1280]{0:T(1024)}, f32[1280]{0:T(1024)S(1)}, u32[]{:S(2)}) copy-start(f32[1280]{0:T(1024)S(1)} %convert_element_type.143) | copy-start | bytes 15364
  176.3 317.9 %copy-start.6 = (f32[2,730]{1,0:T(2,128)}, f32[2,730]{1,0:T(2,128)S(1)}, u32[]{:S(2)}) copy-start(f32[2,730]{1,0:T(2,128)S(1)} %broadcast_multiply_fusion.4) | copy-start | bytes 17524
  179.4 314.9 %copy-start.12 = (f32[2,730]{1,0:T(2,128)}, f32[2,730]{1,0:T(2,128)S(1)}, u32[]{:S(2)}) copy-start(f32[2,730]{1,0:T(2,128)S(1)} %add_rsqrt_fusion) | copy-start | bytes 17524
  219.9 73.3 %copy-start.24 = (f32[1280]{0:T(1024)S(1)}, f32[1280]{0:T(1024)}, u32[]{:S(2)}) copy-start(f32[1280]{0:T(1024)} %convert_element_type.170) | copy-start | bytes 15364
  293.1 27.5 %copy-start.3 = (f32[640,1280]{1,0:T(8,128)S(1)}, f32[640,1280]{1,0:T(8,128)}, u32[]{:S(2)}) copy-start(f32[640,1280]{1,0:T(8,128)} %param.26) | copy-start | bytes 9830404
  322.0 140.7 %all-gather.20.cloned.1.call-start = ((), (), s32[]{:S(2)}) async-start(), calls=%async_computation.9 | async-start | bytes 14745600 | tf_op jit(solution)/shard_map/all_gather | solution.py:100
  325.4 175.2 %all-gather.22.cloned.1.call-start = ((), (), s32[]{:S(2)}) async-start(), calls=%async_computation.10 | async-start | bytes 3686400 | tf_op jit(solution)/shard_map/all_gather | solution.py:100
  327.4 452.8 %all-gather.24.cloned.1.call-start = ((), (), s32[]{:S(2)}) async-start(), calls=%async_computation.11 | async-start | bytes 11059200 | tf_op jit(solution)/shard_map/all_gather | solution.py:100
  354.4 567.0 %all-reduce.22.cloned.1.call-start = ((), (), s32[]{:S(2)}) async-start(), calls=%async_computation.16 | async-start | bytes 172032
  462.7 31.6 %copy-start.1 = (bf16[2,730,1280]{2,1,0:T(8,128)(2,1)S(1)}, bf16[2,730,1280]{2,1,0:T(8,128)(2,1)}, u32[]{:S(2)}) copy-start(bf16[2,730,1280]{2,1,0:T(8,128)(2,1)} %copy-done) | copy-start | bytes 11212804
  462.7 31.6 %copy-start.4 = (bf16[2,730,1280]{2,0,1:T(2,128)(2,1)S(1)}, bf16[2,730,1280]{2,0,1:T(2,128)(2,1)}, u32[]{:S(2)}) copy-start(bf16[2,730,1280]{2,0,1:T(2,128)(2,1)} %param.15) | copy-start | bytes 11212804
  516.7 28.2 %copy-start.39 = (f32[2,16,730]{2,1,0:T(8,128)S(1)}, f32[2,16,730]{2,1,0:T(8,128)}, u32[]{:S(2)}) copy-start(f32[2,16,730]{2,1,0:T(8,128)} %copy-done.38) | copy-start | bytes 280324
  806.5 125.6 %reduce-scatter.7.cloned.1.call-start = ((), (), s32[]{:S(2)}) async-start(), calls=%async_computation.13 | async-start | bytes 7372800 | tf_op jit(solution)/shard_map/reduce_scatter | solution.py:109
  817.6 245.4 %reduce-scatter.11.cloned.1.call-start = ((), (), s32[]{:S(2)}) async-start(), calls=%async_computation.15 | async-start | bytes 29491200 | tf_op jit(solution)/shard_map/reduce_scatter | solution.py:109
  845.2 342.4 %reduce-scatter.5.cloned.1.call-start = ((), (), s32[]{:S(2)}) async-start(), calls=%async_computation.12 | async-start | bytes 22118400 | tf_op jit(solution)/shard_map/reduce_scatter | solution.py:109
  870.2 472.8 %reduce-scatter.9.cloned.1.call-start = ((), (), s32[]{:S(2)}) async-start(), calls=%async_computation.14 | async-start | bytes 29491200 | tf_op jit(solution)/shard_map/reduce_scatter | solution.py:109
  (29 other events, 240.2 us)
Sparse Core Ops, SparseCore 0:
  10.5 58.9 all-gather.9
  71.8 26.8 all-gather.11
  101.2 68.4 all-gather.13
  172.0 68.5 all-gather.15
  322.1 69.7 all-gather.17
  394.1 68.4 all-gather.19
  465.0 26.8 all-gather.21
  494.4 54.6 all-gather.23
  806.6 43.9 all-reduce.21
  854.3 53.2 reduce-scatter.6
  911.8 151.1 reduce-scatter.10
  1067.0 120.5 reduce-scatter.4
  1191.8 151.1 reduce-scatter.8
where the time goes:
time: 1360 us; the launch traced here: 1350 us
  matrix products  596 us (44%)
  waiting for transfers between devices  484 us (36%)
  other arithmetic  136 us (10%)
  blocking collectives  61.4 us (5%)
  local copies, waits for them, and re-layouts  57.5 us (4%)
  between operations  14.8 us (1%)
    reduce_scatter x4, waiting for transfers between devices, device_step(): lax.psum_scatter(grad, 'fsdp', scatter_dimension=0, tiled=True)  411 us
    dot_general x1, matrix products, backward_local(): jnp.einsum('bhqk,bkhd->bqhd', grad_scores, key_heads, preferred_element_t...  91 us
    dot_general x1, matrix products, backward_local(): jnp.einsum('bhqk,bqhd->bkhd', grad_scores, query_heads, preferred_element...  90.9 us
    convert_element_type x1, other arithmetic, forward_local(): hidden = jax.nn.gelu(pre_act, approximate=False).astype(jnp.bfloat16)  73.2 us
    all_gather x8, waiting for transfers between devices, gather_bf16(): lax.all_gather(shard.astype(jnp.bfloat16), 'fsdp', axis=0, tiled=True)  73.2 us
    unnamed x2, blocking collectives  49.1 us
    dot_general x1, matrix products, forward_local(): jnp.einsum('bsw,wf->bsf', normed_two, fc_weight, preferred_element_type=j...  40.4 us
    dot_general x1, matrix products, backward_local(): jnp.einsum('bsw,fw->bsf', grad_out, proj_weight, preferred_element_type=j...  38.3 us
  transfers between devices with their start and end apart: 13, of which 6 were waited for; matrix products, arithmetic and copies ran while one was open for 54% of the time, Pallas kernels for 0%

commit v1 on v0

v1 whole, which is shorter than its diff:
```python
import functools
import math

import jax
import jax.numpy as jnp
from jax import lax
from jax.experimental import pallas as pl
from jax.experimental.pallas import tpu as pltpu
from jax.sharding import PartitionSpec as P

HEADS = 16
HEAD_DIM = 80
GROUP = 8
GROUP_COLS = GROUP * HEAD_DIM
SCALE = HEAD_DIM ** -0.5
LOG2E = math.log2(math.e)
LN_EPS = 1e-5
F32 = jnp.float32
BF16 = jnp.bfloat16
VMEM_LIMIT = 60 * 2 ** 20


def dot(lhs, rhs, lhs_dim, rhs_dim):
    return lax.dot_general(lhs, rhs, (((lhs_dim,), (rhs_dim,)), ((), ())), preferred_element_type=F32)


def attn_fwd_kernel(q_ref, k_ref, v_ref, o_ref, lse_ref):
    for head in range(GROUP):
        cols = slice(head * HEAD_DIM, (head + 1) * HEAD_DIM)
        scores = dot(k_ref[0, :, cols], q_ref[0, :, cols], 1, 1)
        top = jnp.max(scores, axis=0, keepdims=True)
        expo = jnp.exp2((scores - top) * (SCALE * LOG2E))
        total = jnp.sum(expo, axis=0, keepdims=True)
        probs = (expo * (1.0 / total)).astype(BF16)
        o_ref[0, :, cols] = dot(probs, v_ref[0, :, cols], 0, 0).astype(BF16)
        lse_ref[0, 0, head:head + 1, :] = top * (SCALE * LOG2E) + jnp.log2(total)


def attn_bwd_kernel(q_ref, k_ref, v_ref, do_ref, lse_ref, dq_ref, dk_ref, dv_ref):
    for head in range(GROUP):
        cols = slice(head * HEAD_DIM, (head + 1) * HEAD_DIM)
        q, k, v, do = q_ref[0, :, cols], k_ref[0, :, cols], v_ref[0, :, cols], do_ref[0, :, cols]
        scores = dot(k, q, 1, 1)
        probs = jnp.exp2(scores * (SCALE * LOG2E) - lse_ref[0, 0, head:head + 1, :])
        grad_probs = dot(v, do, 1, 1)
        dv_ref[0, :, cols] = dot(probs.astype(BF16), do, 1, 0).astype(BF16)
        delta = jnp.sum(probs * grad_probs, axis=0, keepdims=True)
        grad_scores = (probs * ((grad_probs - delta) * SCALE)).astype(BF16)
        dk_ref[0, :, cols] = dot(grad_scores, q, 1, 0).astype(BF16)
        dq_ref[0, :, cols] = dot(grad_scores, k, 0, 0).astype(BF16)


def attn_specs(qkv):
    images, seq_len, _ = qkv.shape
    groups = qkv.shape[2] // 3 // GROUP_COLS

    def cols(part):
        return pl.BlockSpec((1, seq_len, GROUP_COLS), lambda b, g: (b, 0, part * groups + g))

    lse = pl.BlockSpec((1, 1, GROUP, seq_len), lambda b, g: (b, g, 0, 0))
    return images, seq_len, groups, cols, lse


def attn_fwd(qkv):
    images, seq_len, groups, cols, lse = attn_specs(qkv)
    width = groups * GROUP_COLS
    return pl.pallas_call(
        attn_fwd_kernel, grid=(images, groups), name="attn_fwd",
        in_specs=[cols(0), cols(1), cols(2)], out_specs=[cols(0), lse],
        out_shape=[jax.ShapeDtypeStruct((images, seq_len, width), BF16),
                   jax.ShapeDtypeStruct((images, groups, GROUP, seq_len), F32)],
        cost_estimate=pl.CostEstimate(flops=30 * 10 ** 9, bytes_accessed=16 * 10 ** 6, transcendentals=0),
        compiler_params=pltpu.CompilerParams(vmem_limit_bytes=VMEM_LIMIT))(qkv, qkv, qkv)


def attn_bwd(qkv, grad_mixed, lse_vals):
    images, seq_len, groups, cols, lse = attn_specs(qkv)
    width = groups * GROUP_COLS
    return pl.pallas_call(
        attn_bwd_kernel, grid=(images, groups), name="attn_bwd",
        in_specs=[cols(0), cols(1), cols(2), cols(0), lse], out_specs=[cols(0)] * 3,
        out_shape=[jax.ShapeDtypeStruct((images, seq_len, width), BF16)] * 3,
        cost_estimate=pl.CostEstimate(flops=50 * 10 ** 9, bytes_accessed=30 * 10 ** 6, transcendentals=0),
        compiler_params=pltpu.CompilerParams(vmem_limit_bytes=VMEM_LIMIT))(qkv, qkv, qkv, grad_mixed, lse_vals)


def fc_gelu_kernel(x_ref, w_ref, b_ref, h_ref, slope_ref):
    for image in range(x_ref.shape[0]):
        pre = dot(x_ref[image], w_ref[...], 1, 0) + b_ref[...]
        cdf = 0.5 + 0.5 * lax.erf(pre * (0.5 ** 0.5))
        pdf = jnp.exp2(pre * pre * (-0.5 * LOG2E)) * ((2.0 * math.pi) ** -0.5)
        h_ref[image] = (pre * cdf).astype(BF16)
        slope_ref[image] = cdf + pre * pdf


def fc_gelu(normed, weight, bias, tile=512):
    images, seq_len, width = normed.shape
    ffn = weight.shape[1]
    out = pl.BlockSpec((images, seq_len, tile), lambda j: (0, 0, j))
    return pl.pallas_call(
        fc_gelu_kernel, grid=(ffn // tile,), name="fc_gelu",
        in_specs=[pl.BlockSpec((images, seq_len, width), lambda j: (0, 0, 0)),
                  pl.BlockSpec((width, tile), lambda j: (0, j)), pl.BlockSpec((1, tile), lambda j: (0, j))],
        out_specs=[out, out],
        out_shape=[jax.ShapeDtypeStruct((images, seq_len, ffn), BF16),
                   jax.ShapeDtypeStruct((images, seq_len, ffn), F32)],
        cost_estimate=pl.CostEstimate(flops=30 * 10 ** 9, bytes_accessed=60 * 10 ** 6, transcendentals=0),
        compiler_params=pltpu.CompilerParams(vmem_limit_bytes=VMEM_LIMIT))(normed, weight, bias.reshape(1, ffn))


def layer_norm_fwd(values, gain, bias):
    mean_val = jnp.mean(values, axis=-1, keepdims=True)
    centered = values - mean_val
    inv_std = lax.rsqrt(jnp.mean(centered * centered, axis=-1, keepdims=True) + LN_EPS)
    x_hat = centered * inv_std
    return x_hat * gain + bias, x_hat, inv_std


def layer_norm_bwd(grad_norm, x_hat, inv_std, gain):
    grad_hat = grad_norm * gain
    grad_vals = inv_std * (grad_hat - jnp.mean(grad_hat, axis=-1, keepdims=True)
                           - x_hat * jnp.mean(grad_hat * x_hat, axis=-1, keepdims=True))
    return grad_vals, jnp.sum(grad_norm * x_hat, axis=(0, 1)), jnp.sum(grad_norm, axis=(0, 1))


def einsum(spec, lhs, rhs):
    return jnp.einsum(spec, lhs, rhs, preferred_element_type=F32)


def solution(mesh):
    specs = (P("fsdp"),) * 14
    n = mesh.shape["fsdp"]

    def gather(shard):
        return lax.all_gather(shard.astype(BF16), "fsdp", axis=0, tiled=True)

    def scatter(grad):
        return lax.psum_scatter(grad, "fsdp", scatter_dimension=0, tiled=True)

    def device_step(resid_in, grad_out, ln1_gain, ln1_bias, qkv_weight, qkv_bias, out_weight, out_bias,
                    ln2_gain, ln2_bias, fc_weight, fc_bias, proj_weight, proj_bias):
        vectors = (ln1_gain, ln1_bias, qkv_bias, out_bias, ln2_gain, ln2_bias, fc_bias, proj_bias)
        packed = jnp.concatenate(vectors).astype(BF16)
        packed = lax.all_gather(packed, "fsdp", axis=0)
        full, at = [], 0
        for vec in vectors:
            full.append(packed[:, at:at + vec.shape[0]].reshape(-1))
            at += vec.shape[0]
        ln1_gain, ln1_bias, qkv_bias, out_bias, ln2_gain, ln2_bias, fc_bias, proj_bias = [f.astype(F32) for f in full]
        qkv_weight, out_weight, fc_weight, proj_weight = [gather(w) for w in (qkv_weight, out_weight, fc_weight, proj_weight)]

        resid = resid_in.astype(F32)
        normed, hat_one, inv_one = layer_norm_fwd(resid, ln1_gain, ln1_bias)
        normed_one = normed.astype(BF16)
        qkv = (einsum("bsw,wk->bsk", normed_one, qkv_weight) + qkv_bias).astype(BF16)
        mixed, lse = attn_fwd(qkv)
        middle = (resid + einsum("bsw,wv->bsv", mixed, out_weight) + out_bias).astype(BF16)
        middle_wide = middle.astype(F32)
        normed, hat_two, inv_two = layer_norm_fwd(middle_wide, ln2_gain, ln2_bias)
        normed_two = normed.astype(BF16)
        hidden, slope = fc_gelu(normed_two, fc_weight, fc_bias)
        resid_out = (middle_wide + einsum("bsf,fw->bsw", hidden, proj_weight) + proj_bias).astype(BF16)

        grad_wide = grad_out.astype(F32)
        d_proj_weight = scatter(einsum("bsf,bsw->fw", hidden, grad_out))
        d_proj_bias = jnp.sum(grad_wide, axis=(0, 1))
        grad_pre = einsum("bsw,fw->bsf", grad_out, proj_weight) * slope
        grad_pre_low = grad_pre.astype(BF16)
        d_fc_bias = jnp.sum(grad_pre, axis=(0, 1))
        d_fc_weight = scatter(einsum("bsw,bsf->wf", normed_two, grad_pre_low))
        grad_norm = einsum("bsf,wf->bsw", grad_pre_low, fc_weight)
        grad_ln, d_ln2_gain, d_ln2_bias = layer_norm_bwd(grad_norm, hat_two, inv_two, ln2_gain)
        grad_middle = grad_wide + grad_ln
        grad_middle_low = grad_middle.astype(BF16)
        d_out_weight = scatter(einsum("bsw,bsv->wv", mixed, grad_middle_low))
        d_out_bias = jnp.sum(grad_middle, axis=(0, 1))
        grad_mixed = einsum("bsv,wv->bsw", grad_middle_low, out_weight).astype(BF16)
        parts = attn_bwd(qkv, grad_mixed, lse)
        grad_qkv = jnp.concatenate(parts, axis=-1)
        d_qkv_weight = scatter(einsum("bsw,bsk->wk", normed_one, grad_qkv))
        d_qkv_bias = jnp.sum(grad_qkv.astype(F32), axis=(0, 1))
        grad_norm = einsum("bsk,wk->bsw", grad_qkv, qkv_weight)
        grad_ln, d_ln1_gain, d_ln1_bias = layer_norm_bwd(grad_norm, hat_one, inv_one, ln1_gain)
        grad_in = (grad_middle + grad_ln).astype(BF16)

        small = (d_ln1_gain, d_ln1_bias, d_qkv_bias, d_out_bias, d_ln2_gain, d_ln2_bias, d_fc_bias, d_proj_bias)
        summed = lax.psum_scatter(jnp.concatenate([s.reshape(n, -1) for s in small], axis=1), "fsdp",
                                  scatter_dimension=0, tiled=True).reshape(-1)
        shards, at = [], 0
        for vec in small:
            shards.append(summed[at:at + vec.shape[0] // n])
            at += vec.shape[0] // n
        (d_ln1_gain, d_ln1_bias, d_qkv_bias, d_out_bias, d_ln2_gain, d_ln2_bias, d_fc_bias, d_proj_bias) = shards
        return (resid_out, grad_in, d_ln1_gain, d_ln1_bias, d_qkv_weight, d_qkv_bias, d_out_weight, d_out_bias,
                d_ln2_gain, d_ln2_bias, d_fc_weight, d_fc_bias, d_proj_weight, d_proj_bias)

    return jax.shard_map(device_step, mesh=mesh, in_specs=specs, out_specs=specs, check_vma=False)
```

time: 1360 us -> 957 us (0.70)
  matrix products: 596 us -> 237 us
  Pallas kernels: 0 us -> 129 us
  other arithmetic: 136 us -> 38 us
  blocking collectives: 61.4 us -> 14.7 us
  local copies, waits for them, and re-layouts: 57.5 us -> 28.6 us
    dot_general x17 -> x11, matrix products: 564 us -> 237 us  [einsum(): return jnp.einsum(spec, lhs, rhs, preferred_element_type=F32)]
    pallas_call x0 -> x3, Pallas kernels: none -> 129 us  [the longest x1 59.7 us: attn_bwd(): pl.pallas_call(attn_bwd_kernel, grid=(images, groups), name='attn_bwd', i...]
    convert_element_type x31 -> x8, other arithmetic: 113 us -> 20.9 us  [the longest x4 9.57 us: gather(): return lax.all_gather(shard.astype(BF16), 'fsdp', axis=0, tiled=True)]
    unnamed x2 -> x0, blocking collectives: 49.1 us -> none
    sub x1 -> x0, matrix products: 31.9 us -> none  [forward_local(): attn_probs = jax.nn.softmax(scores, axis=-1)]
    convert_element_type x3 -> x7, local copies, waits for them, and re-layouts: 27.2 us -> 0.52 us  [device_step(): f.astype(F32)]
    all_gather x8 -> x4, waiting for transfers between devices: 73.2 us -> 93.6 us  [gather(): return lax.all_gather(shard.astype(BF16), 'fsdp', axis=0, tiled=True)]
    reduce_scatter x4, waiting for transfers between devices: 411 us -> 394 us  [scatter(): return lax.psum_scatter(grad, 'fsdp', scatter_dimension=0, tiled=True)]
  transfers between devices with their start and end apart: 13 -> 9, of which waited for: 6 -> 6; matrix products, arithmetic and copies ran while one was open for 54% -> 20% of each run, Pallas kernels for 0% -> 7%
where the time goes in v1:
time: 957 us; the launch traced here: 951 us
  waiting for transfers between devices  488 us (51%)
  matrix products  237 us (25%)
  Pallas kernels  129 us (13%)
  other arithmetic  38 us (4%)
  local copies, waits for them, and re-layouts  28.6 us (3%)
  between operations  14.9 us (2%)
  blocking collectives  14.7 us (2%)
    reduce_scatter x4, waiting for transfers between devices, scatter(): return lax.psum_scatter(grad, 'fsdp', scatter_dimension=0, tiled=True)  394 us
    dot_general x11, matrix products, einsum(): return jnp.einsum(spec, lhs, rhs, preferred_element_type=F32)  237 us
    all_gather x4, waiting for transfers between devices, gather(): return lax.all_gather(shard.astype(BF16), 'fsdp', axis=0, tiled=True)  93.6 us
    pallas_call x1, Pallas kernels, attn_bwd(): pl.pallas_call(attn_bwd_kernel, grid=(images, groups), name='attn_bwd', i...  59.7 us
    pallas_call x1, Pallas kernels, attn_fwd(): pl.pallas_call(attn_fwd_kernel, grid=(images, groups), name='attn_fwd', i...  35.7 us
    pallas_call x1, Pallas kernels, fc_gelu(): pl.pallas_call(fc_gelu_kernel, grid=(ffn // tile,), name='fc_gelu', in_sp...  34.1 us
    unnamed x60, local copies, waits for them, and re-layouts  20.2 us
  transfers between devices with their start and end apart: 9, of which 6 were waited for; matrix products, arithmetic and copies ran while one was open for 20% of the time, Pallas kernels for 7%

profile of v1, /device:TPU:0, one launch (start us, length us, event | category | flops | bytes accessed | tf_op | source)
XLA Modules:
  0.0 950.8 jit_solution(4581190160237555922)
XLA Ops:
  17.6 14.7 %all-gather = bf16[8,1,2080]{2,1,0:T(2,128)(2,1)S(1)} all-gather(bf16[1,1,2080]{2,1,0:T(2,128)(2,1)S(1)} %bitcast.63), channel_id=1, replica_groups=mesh['fsdp'=8] {'fsdp'}, dimensions={0}, use_global_device_ids=true | all-gather | bytes 37440 | tf_op jit(solution)/shard_map/all_gather | solution.py:144
  39.8 28.9 %all-gather.6.cloned.1.call-done = bf16[1280,3840]{1,0:T(8,128)(2,1)} async-done(((bf16[160,3840]{1,0:T(8,128)(2,1)}), bf16[1280,3840]{1,0:T(8,128)(2,1)}) %all-gather.6.cloned.1.call-update) | async-done | bytes 9830416 | tf_op jit(solution)/shard_map/all_gather | solution.py:135
  68.7 22.2 %add_convert_fusion.q_ref.k_ref.v_ref = bf16[2,730,3840]{2,1,0:T(8,128)(2,1)} fusion(f32[3840]{0:T(1024)S(1)} %reshape.296, bf16[1280,3840]{1,0:T(8,128)(2,1)} %all-gather.6.cloned.1.call-done, f32[1280]{0:T(1024)S(1)} %reshape.295, f32[1280]{0:T(1024)S(1)} %reshape.294, f32[2,730]{1,0:T(2,128)S(1)} %add_rsqrt_fusion.1, ...), kind=kOutput, calls=%fused_computation.1 | convolution fusion | flops 14374809600 | bytes 24818080 | tf_op jit(solution)/shard_map/bsw,wk->bsk/dot_general | solution.py:127
  90.9 35.7 %attn_fwd.1 = (bf16[2,730,1280]{2,1,0:T(8,128)(2,1)}, f32[2,2,8,730]{3,2,1,0:T(8,128)}) custom-call(bf16[2,730,3840]{2,1,0:T(8,128)(2,1)} %add_convert_fusion.q_ref.k_ref.v_ref, bf16[2,730,3840]{2,1,0:T(8,128)(2,1)} %add_convert_fusion.q_ref.k_ref.v_ref, bf16[2,730,3840]{2,1,0:T(8,128)(2,1)} %add_convert_fusion.q_ref.k_ref.v_ref), custom_call_target="tpu_custom_call" | custom-call | flops 30000001024 | bytes 16000000 | tf_op jit(solution)/shard_map/attn_fwd/pallas_call | solution.py:67
  126.6 9.7 %convert_reduce_fusion.1 = (f32[2,730]{1,0:T(2,128)S(1)}, bf16[2,730,1280]{2,1,0:T(8,128)(2,1)S(1)}) fusion(f32[1280]{0:T(1024)S(1)} %reshape.297, bf16[2,730,1280]{2,1,0:T(8,128)(2,1)} %get-tuple-element.21, bf16[1280,1280]{1,0:T(8,128)(2,1)} %all-gather.8.cloned.1.call-done, bf16[2,730,1280]{2,0,1:T(2,128)(2,1)} %param.14), kind=kOutput, calls=%fused_computation.13 | convolution fusion | flops 4795339264 | bytes 14500560 | tf_op jit(solution)/shard_map/bsw,wv->bsv/dot_general | solution.py:127
  141.0 27.9 %all-gather.10.cloned.1.call-done.w_ref = bf16[1280,5120]{1,0:T(8,128)(2,1)} async-done(((bf16[160,5120]{1,0:T(8,128)(2,1)}), bf16[1280,5120]{1,0:T(8,128)(2,1)}) %all-gather.10.cloned.1.call-update) | async-done | bytes 13107216 | tf_op jit(solution)/shard_map/all_gather | solution.py:135
  168.9 34.1 %fc_gelu.1 = (bf16[2,730,5120]{2,1,0:T(8,128)(2,1)}, f32[2,730,5120]{2,1,0:T(8,128)}) custom-call(bf16[2,730,1280]{2,1,0:T(8,128)(2,1)} %fusion.21.x_ref, bf16[1280,5120]{1,0:T(8,128)(2,1)} %all-gather.10.cloned.1.call-done.w_ref, f32[1,5120]{1,0:T(1,128)} %bitcast.64), custom_call_target="tpu_custom_call" | custom-call | flops 30000001024 | bytes 60000000 | tf_op jit(solution)/shard_map/fc_gelu/pallas_call | solution.py:100
  203.0 36.7 %all-gather.12.cloned.1.call-done = bf16[5120,1280]{1,0:T(8,128)(2,1)} async-done(((bf16[640,1280]{1,0:T(8,128)(2,1)}), bf16[5120,1280]{1,0:T(8,128)(2,1)}) %all-gather.12.cloned.1.call-update) | async-done | bytes 13107216 | tf_op jit(solution)/shard_map/all_gather | solution.py:135
  239.7 28.5 %fusion.56 = (f32[5120]{0:T(1024)S(1)}, bf16[2,730,5120]{2,1,0:T(8,128)(2,1)}) fusion(f32[2,730,5120]{2,1,0:T(8,128)} %get-tuple-element.23, bf16[5120,1280]{1,0:T(8,128)(2,1)} %all-gather.12.cloned.1.call-done, bf16[2,730,1280]{2,0,1:T(2,128)(2,1)} %param.15), kind=kOutput, calls=%fused_computation.92 | convolution fusion | flops 19158933504 | bytes 61716480 | tf_op jit(solution)/shard_map/bsw,fw->bsf/dot_general | solution.py:127
  268.2 30.8 %fusion.25 = (f32[1280]{0:T(1024)S(1)}, f32[2,730]{1,0:T(2,128)S(1)}, f32[2,730]{1,0:T(2,128)S(1)}, f32[1280]{0:T(1024)S(1)}, f32[2,730,1280]{2,1,0:T(8,128)S(1)}) fusion(bf16[2,730,1280]{2,1,0:T(8,128)(2,1)S(1)} %copy-done.1, f32[2,730]{1,0:T(2,128)S(1)} %add_rsqrt_fusion, f32[2,730]{1,0:T(2,128)S(1)} %broadcast_multiply_fusion.4, f32[1280]{0:T(1024)S(1)} %reshape.298, ...), kind=kOutput, calls=%fused_computation.40 | convolution fusion | flops 19155189760 | bytes 39309120 | tf_op jit(solution)/shard_map/bsf,wf->bsw/dot_general | solution.py:127
  303.3 6.6 convolution_convert_fusion.do_ref
  309.9 59.7 %attn_bwd.1 = (bf16[2,730,1280]{2,1,0:T(8,128)(2,1)}, bf16[2,730,1280]{2,1,0:T(8,128)(2,1)}, bf16[2,730,1280]{2,1,0:T(8,128)(2,1)}) custom-call(bf16[2,730,3840]{2,1,0:T(8,128)(2,1)} %add_convert_fusion.q_ref.k_ref.v_ref, bf16[2,730,3840]{2,1,0:T(8,128)(2,1)} %add_convert_fusion.q_ref.k_ref.v_ref, bf16[2,730,3840]{2,1,0:T(8,128)(2,1)} %add_convert_fusion.q_ref.k_ref.v_ref, ...), custom_call_target="tpu_custom_call" | custom-call | flops 49999998976 | bytes 30000000 | tf_op jit(solution)/shard_map/attn_bwd/pallas_call | solution.py:79
  378.5 6.0 convert_reduce_fusion
  384.5 23.2 %fusion.34 = (f32[1280]{0:T(1024)S(1)}, f32[2,730]{1,0:T(2,128)S(1)}, f32[2,730]{1,0:T(2,128)S(1)}, f32[1280]{0:T(1024)S(1)}, f32[2,730,1280]{2,1,0:T(8,128)}) fusion(f32[2,730]{1,0:T(2,128)S(1)} %copy-done.15, f32[2,730]{1,0:T(2,128)S(1)} %copy-done.10, bf16[2,730,1280]{2,0,1:T(2,128)(2,1)S(1)} %copy-done.3, f32[1280]{0:T(1024)S(1)} %copy-done.12, ...), kind=kOutput, calls=%fused_computation.49 | convolution fusion | flops 14371067904 | bytes 32294720 | tf_op jit(solution)/shard_map/bsk,wk->bsw/dot_general | solution.py:127
  409.0 11.0 %convolution_bitcast_fusion.3 = f32[1280,1280]{1,0:T(8,128)} fusion(bf16[2,730,1280]{2,1,0:T(8,128)(2,1)} %get-tuple-element.21, f32[2,730,1280]{2,1,0:T(8,128)} %copy-done.4), kind=kOutput, calls=%fused_computation.34 | convolution fusion | flops 4785996800 | bytes 17766400 | tf_op jit(solution)/shard_map/bsw,bsv->wv/dot_general | solution.py:127
  420.1 23.6 %convolution_bitcast_fusion.2 = f32[1280,3840]{1,0:T(8,128)} fusion(bf16[2,730,3840]{2,1,0:T(8,128)(2,1)} %constant_dynamic-update-slice_fusion, f32[1280]{0:T(1024)S(1)} %copy-done.17, f32[1280]{0:T(1024)S(1)} %copy-done.12, f32[2,730]{1,0:T(2,128)S(1)} %copy-done.15, f32[2,730]{1,0:T(2,128)S(1)} %copy-done.10, bf16[2,730,1280]{2,0,1:T(2,128)(2,1)} %param.14), kind=kOutput, calls=%fused_computation.4 | convolution fusion | flops 14363596800 | bytes 34633120 | tf_op jit(solution)/shard_map/bsw,bsk->wk/dot_general | solution.py:127
  443.8 27.4 %convolution_bitcast_fusion.1 = f32[1280,5120]{1,0:T(8,128)} fusion(bf16[2,730,1280]{2,1,0:T(8,128)(2,1)} %fusion.21.x_ref, bf16[2,730,5120]{2,1,0:T(8,128)(2,1)} %get-tuple-element.98), kind=kOutput, calls=%fused_computation.3 | convolution fusion | flops 19136512000 | bytes 44902400 | tf_op jit(solution)/shard_map/bsw,bsf->wf/dot_general | solution.py:127
  471.2 27.6 %convolution_bitcast_fusion = f32[5120,1280]{1,0:T(8,128)} fusion(bf16[2,730,5120]{2,1,0:T(8,128)(2,1)} %get-tuple-element.22, bf16[2,730,1280]{2,0,1:T(2,128)(2,1)} %param.15), kind=kOutput, calls=%fused_computation.2 | convolution fusion | flops 19136512000 | bytes 44902400 | tf_op jit(solution)/shard_map/bsf,bsw->fw/dot_general | solution.py:127
  499.6 7.9 fusion.33
  507.5 5.7 copy.45
  513.2 26.3 %fusion.39 = bf16[2,730,1280]{2,1,0:T(8,128)(2,1)S(1)} fusion(bf16[2,730,1280]{2,1,0:T(8,128)(2,1)S(1)} %copy-done.2, bf16[2,730,5120]{2,1,0:T(8,128)(2,1)} %get-tuple-element.22, bf16[5120,1280]{1,0:T(8,128)(2,1)} %all-gather.12.cloned.1.call-done, f32[1280]{0:T(1024)S(1)} %reshape.301), kind=kOutput, calls=%fused_computation.54 | convolution fusion | flops 19143983104 | bytes 35537920 | tf_op jit(solution)/shard_map/bsf,fw->bsw/dot_general | solution.py:127
  549.5 83.7 %reduce-scatter.5.cloned.1.call-done = f32[160,3840]{1,0:T(8,128)} async-done(((f32[1280,3840]{1,0:T(8,128)}), f32[160,3840]{1,0:T(8,128)}) %reduce-scatter.5.cloned.1.call-update) | async-done | bytes 2457616 | tf_op jit(solution)/shard_map/reduce_scatter | solution.py:138
  633.1 155.3 %reduce-scatter.9.cloned.1.call-done = f32[160,5120]{1,0:T(8,128)} async-done(((f32[1280,5120]{1,0:T(8,128)}), f32[160,5120]{1,0:T(8,128)}) %reduce-scatter.9.cloned.1.call-update) | async-done | bytes 3276816 | tf_op jit(solution)/shard_map/reduce_scatter | solution.py:138
  788.5 155.4 %reduce-scatter.11.cloned.1.call-done = f32[640,1280]{1,0:T(8,128)} async-done(((f32[5120,1280]{1,0:T(8,128)}), f32[640,1280]{1,0:T(8,128)}) %reduce-scatter.11.cloned.1.call-update) | async-done | bytes 3276816 | tf_op jit(solution)/shard_map/reduce_scatter | solution.py:138
  (136 shorter events, 47.6 us)
Async XLA Ops:
  7.2 61.5 %all-gather.6.cloned.1.call-start = ((), (), s32[]{:S(2)}) async-start(), calls=%async_computation.4 | async-start | bytes 11059200 | tf_op jit(solution)/shard_map/all_gather | solution.py:135
  10.3 7.0 copy-start.19
  10.3 7.0 copy-start.21
  10.3 7.0 copy-start.22
  10.3 7.0 copy-start.23
  10.3 7.1 copy-start.24
  10.3 7.1 copy-start.25
  10.3 7.1 copy-start.26
  10.4 116.3 %all-gather.8.cloned.1.call-start = ((), (), s32[]{:S(2)}) async-start(), calls=%async_computation.5 | async-start | bytes 3686400 | tf_op jit(solution)/shard_map/all_gather | solution.py:135
  12.4 156.5 %all-gather.10.cloned.1.call-start = ((), (), s32[]{:S(2)}) async-start(), calls=%async_computation.6 | async-start | bytes 14745600 | tf_op jit(solution)/shard_map/all_gather | solution.py:135
  13.8 225.9 %all-gather.12.cloned.1.call-start = ((), (), s32[]{:S(2)}) async-start(), calls=%async_computation.7 | async-start | bytes 14745600 | tf_op jit(solution)/shard_map/all_gather | solution.py:135
  17.2 528.0 %all-reduce.3.cloned.1.call-start = ((), (), s32[]{:S(2)}) async-start(), calls=%async_computation.12 | async-start | bytes 139264
  33.0 57.9 %copy-start.11 = (f32[1280]{0:T(1024)}, f32[1280]{0:T(1024)S(1)}, u32[]{:S(2)}) copy-start(f32[1280]{0:T(1024)S(1)} %reshape.294) | copy-start | bytes 15364
  33.0 57.8 %copy-start.16 = (f32[1280]{0:T(1024)}, f32[1280]{0:T(1024)S(1)}, u32[]{:S(2)}) copy-start(f32[1280]{0:T(1024)S(1)} %reshape.295) | copy-start | bytes 15364
  36.6 54.3 %copy-start.9 = (f32[2,730]{1,0:T(2,128)}, f32[2,730]{1,0:T(2,128)S(1)}, u32[]{:S(2)}) copy-start(f32[2,730]{1,0:T(2,128)S(1)} %broadcast_multiply_fusion.5) | copy-start | bytes 17524
  39.8 51.1 %copy-start.14 = (f32[2,730]{1,0:T(2,128)}, f32[2,730]{1,0:T(2,128)S(1)}, u32[]{:S(2)}) copy-start(f32[2,730]{1,0:T(2,128)S(1)} %add_rsqrt_fusion.1) | copy-start | bytes 17524
  239.7 28.5 %copy-start.1 = (bf16[2,730,1280]{2,1,0:T(8,128)(2,1)S(1)}, bf16[2,730,1280]{2,1,0:T(8,128)(2,1)}, u32[]{:S(2)}) copy-start(bf16[2,730,1280]{2,1,0:T(8,128)(2,1)} %copy-done) | copy-start | bytes 11212804
  268.2 30.9 %copy-start.7 = (bf16[2,730,1280]{2,0,1:T(2,128)(2,1)S(1)}, bf16[2,730,1280]{2,0,1:T(2,128)(2,1)}, u32[]{:S(2)}) copy-start(bf16[2,730,1280]{2,0,1:T(2,128)(2,1)} %param.15) | copy-start | bytes 11212804
  409.0 11.1 %copy-start.17 = (f32[1280]{0:T(1024)S(1)}, f32[1280]{0:T(1024)}, u32[]{:S(2)}) copy-start(f32[1280]{0:T(1024)} %copy-done.16) | copy-start | bytes 15364
  409.0 140.5 %reduce-scatter.7.cloned.1.call-start = ((), (), s32[]{:S(2)}) async-start(), calls=%async_computation.9 | async-start | bytes 7372800 | tf_op jit(solution)/shard_map/reduce_scatter | solution.py:138
  420.0 213.1 %reduce-scatter.5.cloned.1.call-start = ((), (), s32[]{:S(2)}) async-start(), calls=%async_computation.8 | async-start | bytes 22118400 | tf_op jit(solution)/shard_map/reduce_scatter | solution.py:138
  443.7 344.8 %reduce-scatter.9.cloned.1.call-start = ((), (), s32[]{:S(2)}) async-start(), calls=%async_computation.10 | async-start | bytes 29491200 | tf_op jit(solution)/shard_map/reduce_scatter | solution.py:138
  471.2 472.7 %reduce-scatter.11.cloned.1.call-start = ((), (), s32[]{:S(2)}) async-start(), calls=%async_computation.11 | async-start | bytes 29491200 | tf_op jit(solution)/shard_map/reduce_scatter | solution.py:138
  499.6 13.6 %copy-start.2 = (bf16[2,730,1280]{2,1,0:T(8,128)(2,1)S(1)}, bf16[2,730,1280]{2,1,0:T(8,128)(2,1)}, u32[]{:S(2)}) copy-start(bf16[2,730,1280]{2,1,0:T(8,128)(2,1)} %copy-done) | copy-start | bytes 11212804
  (12 other events, 60.8 us)
Sparse Core Ops, SparseCore 0:
  10.4 58.2 all-gather.5
  71.0 26.8 all-gather.7
  100.4 68.4 all-gather.9
  171.2 68.4 all-gather.11
  409.1 42.0 all-reduce.2
  455.0 53.3 reduce-scatter.6
  512.6 120.5 reduce-scatter.4
  637.3 151.1 reduce-scatter.8
  792.7 151.1 reduce-scatter.10
